TPU v7x, 32 devices: a whole 2x2x4 slice. The times are simulated.
32 devices in a mesh: replica: 8 (over y, x, core), model: 4 (over z).
Axes of the slice: x: 2, y: 2, z: 4, core: 2. Of those that a mesh axis runs over, the one named last changes fastest.
Arguments:
- slope_gate: float32 [8, 2048, 6144], P('replica', None, 'model'), may hold values from -0.875 to 0.875
- slope_up: float32 [8, 2048, 6144], P('replica', None, 'model'), may hold values from -0.875 to 0.875
- slope_down: float32 [8, 6144, 2048], P('replica', 'model'), may hold values from -0.875 to 0.875
- slope_norm: float32 [8, 2048], P('replica'), may hold values from -8 to 8
- param_gate: float32 [2048, 6144], P('replica', 'model'), may hold values from -0.1875 to 0.1875
- param_up: float32 [2048, 6144], P('replica', 'model'), may hold values from -0.1875 to 0.1875
- param_down: float32 [6144, 2048], P('model', 'replica'), may hold values from -0.109375 to 0.109375
- param_norm: float32 [2048], P('replica'), may hold values from 0.25 to 1.75
Outputs:
- half_gate: bfloat16 [2048, 6144], P(None, 'model')
- half_up: bfloat16 [2048, 6144], P(None, 'model')
- half_down: bfloat16 [6144, 2048], P('model')
- half_norm: bfloat16 [2048], replicated
- next_gate: float32 [2048, 6144], P('replica', 'model')
- next_up: float32 [2048, 6144], P('replica', 'model')
- next_down: float32 [6144, 2048], P('model', 'replica')
- next_norm: float32 [2048], P('replica')
All inputs are finite; a program needn't handle non-finite values.
Results may differ from a plain program's by a relative error of at most 0.0004.
Values may be sent and summed in bfloat16 or wider, within the bound.
A program may use at most 128 MiB of HBM per device.

v0:
```python
import jax
import jax.numpy as jnp
from jax import lax
from jax.sharding import PartitionSpec as P

learn_rate = 0.5


def body(
    slope_gate, slope_up, slope_down, slope_norm, param_gate, param_up, param_down, param_norm
):
    mean_gate, mean_up, mean_down = (
        lax.psum_scatter(slope_gate[0], "replica", scatter_dimension=0, tiled=True),
        lax.psum_scatter(slope_up[0], "replica", scatter_dimension=0, tiled=True),
        lax.psum_scatter(slope_down[0], "replica", scatter_dimension=1, tiled=True),
    )
    whole_norm = lax.psum(slope_norm[0], "replica")
    place = lax.axis_index("replica")
    mean_norm = lax.dynamic_slice_in_dim(
        whole_norm, place * param_norm.shape[0], param_norm.shape[0]
    )
    mean_rate = lax.axis_size("replica") ** (-0.5)
    mean_gate = mean_gate * mean_rate
    mean_up = mean_up * mean_rate
    mean_down = mean_down * mean_rate
    mean_norm = mean_norm * mean_rate
    own_gate, own_up, own_down, slope_gate_norm, slope_up_norm, slope_down_norm = lax.psum(
        (
            jnp.sum(param_gate * param_gate, axis=1, keepdims=True),
            jnp.sum(param_up * param_up, axis=1, keepdims=True),
            jnp.sum(param_down * param_down, axis=0, keepdims=True),
            jnp.sum(mean_gate * mean_gate, axis=1, keepdims=True),
            jnp.sum(mean_up * mean_up, axis=1, keepdims=True),
            jnp.sum(mean_down * mean_down, axis=0, keepdims=True),
        ),
        "model",
    )
    mean_gate = mean_gate * (jnp.sqrt(own_gate) * lax.rsqrt(slope_gate_norm + 1e-06))
    mean_up = mean_up * (jnp.sqrt(own_up) * lax.rsqrt(slope_up_norm + 1e-06))
    mean_down = mean_down * (jnp.sqrt(own_down) * lax.rsqrt(slope_down_norm + 1e-06))
    next_gate = param_gate - learn_rate * mean_gate
    next_up = param_up - learn_rate * mean_up
    next_down = param_down - learn_rate * mean_down
    next_norm = param_norm - learn_rate * mean_norm
    half_gate, half_up, half_down, half_norm = (
        lax.all_gather(next_gate.astype(jnp.bfloat16), "replica", axis=0, tiled=True),
        lax.all_gather(next_up.astype(jnp.bfloat16), "replica", axis=0, tiled=True),
        lax.all_gather(next_down.astype(jnp.bfloat16), "replica", axis=1, tiled=True),
        lax.all_gather(next_norm.astype(jnp.bfloat16), "replica", axis=0, tiled=True),
    )
    return (half_gate, half_up, half_down, half_norm, next_gate, next_up, next_down, next_norm)


def solution(mesh):
    return jax.shard_map(
        body,
        mesh=mesh,
        in_specs=(
            P("replica", None, "model"),
            P("replica", None, "model"),
            P("replica", "model", None),
            P("replica", None),
            P("replica", "model"),
            P("replica", "model"),
            P("model", "replica"),
            P("replica"),
        ),
        out_specs=(
            P(None, "model"),
            P(None, "model"),
            P("model", None),
            P(),
            P("replica", "model"),
            P("replica", "model"),
            P("model", "replica"),
            P("replica"),
        ),
        check_vma=False,
    )
```

profile of v0, /device:TPU:0, one launch (start us, length us, event | category | flops | bytes accessed | tf_op | source)
XLA Modules:
  0.0 474.7 jit_solution(13732706785687621604)
XLA Ops:
  7.2 0.7 reduce-scatter.8.cloned.1.call-update
  7.9 0.7 reduce-scatter.4.cloned.1.call-update
  8.7 0.7 reduce-scatter.6.cloned.1.call-update
  9.4 0.7 copy-done.2
  10.1 0.2 multiply_reduce_fusion.5
  10.3 0.6 copy-done.1
  10.9 0.2 multiply_reduce_fusion.3
  11.1 0.5 copy-done.3
  11.6 0.2 multiply_reduce_fusion.1
  11.9 94.3 %reduce-scatter.8.cloned.1.call-done = f32[1536,256]{1,0:T(8,128)} async-done(((f32[1536,2048]{1,0:T(8,128)}), f32[1536,256]{1,0:T(8,128)}) %reduce-scatter.8.cloned.1.call-update) | async-done | bytes 1572880 | tf_op jit(solution)/shard_map/reduce_scatter | solution.py:15
  106.2 1.6 multiply_reduce_fusion
  107.8 94.1 %reduce-scatter.4.cloned.1.call-done = f32[256,1536]{1,0:T(8,128)} async-done(((f32[2048,1536]{1,0:T(8,128)}), f32[256,1536]{1,0:T(8,128)}) %reduce-scatter.4.cloned.1.call-update) | async-done | bytes 1572880 | tf_op jit(solution)/shard_map/reduce_scatter | solution.py:13
  202.0 1.6 multiply_reduce_fusion.4
  203.6 94.2 %reduce-scatter.6.cloned.1.call-done = f32[256,1536]{1,0:T(8,128)} async-done(((f32[2048,1536]{1,0:T(8,128)}), f32[256,1536]{1,0:T(8,128)}) %reduce-scatter.6.cloned.1.call-update) | async-done | bytes 1572880 | tf_op jit(solution)/shard_map/reduce_scatter | solution.py:14
  297.8 1.6 multiply_reduce_fusion.2
  299.4 11.9 %all-reduce = (f32[256,1]{0,1:T(1,128)S(1)}, f32[256,1]{0,1:T(1,128)S(1)}, f32[256,1]{0,1:T(1,128)S(1)}, f32[256,1]{0,1:T(1,128)S(1)}, f32[1,256]{1,0:T(1,128)S(1)}, /*index=5*/f32[1,256]{1,0:T(1,128)S(1)}) all-reduce(f32[256,1]{0,1:T(1,128)S(1)} %bitcast.30, ...), channel_id=1, replica_groups=mesh['replica'=8,'model'=4] {'model'}, use_global_device_ids=true, to_apply=%region_4.0 | all-reduce | flops 1536 | bytes 12288 | tf_op jit(solution)/shard_map/psum | solution.py:27
  311.4 3.1 fusion.2
  314.4 0.0 all-gather.5.cloned.1.call-start
  314.5 3.2 fusion.3
  317.7 0.0 all-gather.9.cloned.1.call-start
  317.8 3.2 fusion.1
  321.0 12.8 %psum.55 = f32[2048]{0:T(1024)S(1)} all-reduce(f32[2048]{0:T(1024)S(1)} %bitcast.21), channel_id=1, replica_groups=mesh['replica'=8,'model'=4] {'replica'}, use_global_device_ids=true, to_apply=%region_15.0 | all-reduce | flops 2048 | bytes 16384 | tf_op jit(solution)/shard_map/psum | solution.py:17
  333.8 0.6 fusion
  334.5 9.0 %all-gather = bf16[8,1,256]{2,1,0:T(2,128)(2,1)S(1)} all-gather(bf16[1,1,256]{2,1,0:T(2,128)(2,1)S(1)} %reshape.22), channel_id=1, replica_groups=mesh['replica'=8,'model'=4] {'replica'}, dimensions={0}, use_global_device_ids=true | all-gather | bytes 4608 | tf_op jit(solution)/shard_map/all_gather | solution.py:49
  343.5 0.6 copy.16
  344.1 13.3 %all-gather.7.cloned.1.call-done = bf16[2048,1536]{1,0:T(8,128)(2,1)} async-done(((bf16[256,1536]{1,0:T(8,128)(2,1)}), bf16[2048,1536]{1,0:T(8,128)(2,1)}) %all-gather.7.cloned.1.call-update) | async-done | bytes 6291472 | tf_op jit(solution)/shard_map/all_gather | solution.py:47
  357.4 47.7 %all-gather.5.cloned.1.call-done = bf16[2048,1536]{1,0:T(8,128)(2,1)} async-done(((bf16[256,1536]{1,0:T(8,128)(2,1)}), bf16[2048,1536]{1,0:T(8,128)(2,1)}) %all-gather.5.cloned.1.call-update) | async-done | bytes 6291472 | tf_op jit(solution)/shard_map/all_gather | solution.py:46
  405.1 48.9 %all-gather.9.cloned.1.call-done = bf16[1536,2048]{1,0:T(8,128)(2,1)} async-done(((bf16[1536,256]{1,0:T(8,128)(2,1)}), bf16[1536,2048]{1,0:T(8,128)(2,1)}) %all-gather.9.cloned.1.call-update) | async-done | bytes 6291472 | tf_op jit(solution)/shard_map/all_gather | solution.py:48
  454.0 6.5 %copy.20 = bf16[2048,1536]{1,0:T(8,128)(2,1)} copy(bf16[2048,1536]{1,0:T(8,128)(2,1)} %all-gather.5.cloned.1.call-done) | data formatting | bytes 12582912
  460.6 3.2 copy.21
  463.8 1.4 slice-done.1
  465.1 2.7 copy.22
  (26 shorter events, 0.3 us)
Async XLA Ops:
  7.2 99.0 %reduce-scatter.8.cloned.1.call-start = ((), (), s32[]{:S(2)}) async-start(), calls=%async_computation.7 | async-start | bytes 14155776 | tf_op jit(solution)/shard_map/reduce_scatter | solution.py:15
  7.9 194.1 %reduce-scatter.4.cloned.1.call-start = ((), (), s32[]{:S(2)}) async-start(), calls=%async_computation.3 | async-start | bytes 14155776 | tf_op jit(solution)/shard_map/reduce_scatter | solution.py:13
  8.7 289.1 %reduce-scatter.6.cloned.1.call-start = ((), (), s32[]{:S(2)}) async-start(), calls=%async_computation.5 | async-start | bytes 14155776 | tf_op jit(solution)/shard_map/reduce_scatter | solution.py:14
  8.7 1.4 copy-start.2
  9.4 1.5 copy-start.1
  9.4 348.0 %all-gather.7.cloned.1.call-start = ((), (), s32[]{:S(2)}) async-start(), calls=%async_computation.6 | async-start | bytes 7077888 | tf_op jit(solution)/shard_map/all_gather | solution.py:47
  10.1 1.5 copy-start.3
  314.4 90.7 %all-gather.5.cloned.1.call-start = ((), (), s32[]{:S(2)}) async-start(), calls=%async_computation.4 | async-start | bytes 7077888 | tf_op jit(solution)/shard_map/all_gather | solution.py:46
  314.5 3.3 copy-start.4
  317.7 136.3 %all-gather.9.cloned.1.call-start = ((), (), s32[]{:S(2)}) async-start(), calls=%async_computation.8 | async-start | bytes 7077888 | tf_op jit(solution)/shard_map/all_gather | solution.py:48
  317.8 3.3 copy-start.5
  317.8 16.0 %copy-start.6 = (f32[256]{0:T(256)S(1)}, f32[256]{0:T(256)}, u32[]{:S(2)}) copy-start(f32[256]{0:T(256)} %param.15) | copy-start | bytes 3076
  454.0 6.6 %copy-start = (bf16[2048,1536]{1,0:T(8,128)(2,1)S(1)}, bf16[2048,1536]{1,0:T(8,128)(2,1)}, u32[]{:S(2)}) copy-start(bf16[2048,1536]{1,0:T(8,128)(2,1)} %all-gather.7.cloned.1.call-done) | copy-start | bytes 18874372
  454.0 9.8 %slice-start = ((s8[6291456]{0:T(1024)(128)(4,1)}), s8[4194304]{0:T(1024)(128)(4,1)S(1)}, s32[]{:S(2)}) async-start(s8[6291456]{0:T(1024)(128)(4,1)} %bitcast.18), calls=%async_computation.9 | async-start | bytes 8388608
  460.6 4.6 slice-start.1
Sparse Core Ops, SparseCore 0:
  11.5 94.6 reduce-scatter.7
  109.7 92.2 reduce-scatter.3
  205.5 92.2 reduce-scatter.5
  314.6 42.7 all-gather.6
  359.7 45.3 all-gather.4
  407.4 46.5 all-gather.8
where the time goes:
time: 475 us
  waiting for transfers between devices  395 us (83%)
  blocking collectives  33.6 us (7%)
  local copies, waits for them, and re-layouts  16.3 us (3%)
  other arithmetic  15.7 us (3%)
  between operations  14.2 us (3%)
    reduce_scatter x1, waiting for transfers between devices, body(): lax.psum_scatter(slope_down[0], 'replica', scatter_dimension=1, tiled=True)  94.3 us
    reduce_scatter x1, waiting for transfers between devices, body(): lax.psum_scatter(slope_up[0], 'replica', scatter_dimension=0, tiled=True)  94.2 us
    reduce_scatter x1, waiting for transfers between devices, body(): lax.psum_scatter(slope_gate[0], 'replica', scatter_dimension=0, tiled=True)  94.1 us
    all_gather x1, waiting for transfers between devices, body(): lax.all_gather(next_down.astype(jnp.bfloat16), 'replica', axis=1, tiled=T...  48.9 us
    all_gather x1, waiting for transfers between devices, body(): lax.all_gather(next_gate.astype(jnp.bfloat16), 'replica', axis=0, tiled=T...  47.7 us
    unnamed x23, local copies, waits for them, and re-layouts  16.3 us
    all_gather x1, waiting for transfers between devices, body(): lax.all_gather(next_up.astype(jnp.bfloat16), 'replica', axis=0, tiled=True)  13.3 us
    psum x1, blocking collectives, body(): whole_norm = lax.psum(slope_norm[0], 'replica')  12.8 us
  transfers between devices with their start and end apart: 6, of which 6 were waited for; matrix products, arithmetic and copies ran while one was open for 2% of the time, Pallas kernels for 0%

commit v1 on v0

v1 whole, which is shorter than its diff:
```python
import functools

import jax
import jax.numpy as jnp
from jax import lax
from jax.experimental import pallas as pl
from jax.experimental.pallas import tpu as pltpu
from jax.sharding import PartitionSpec as P

learn_rate = 0.5
eps = 1e-06
MESH = pl.DeviceIdType.MESH
f32, bf16 = jnp.float32, jnp.bfloat16
PIECES = 2
SLOTS = 4


def tile_rows(columns, most=12288):
    return 8 * max(1, most // (8 * columns))


def kernel(
    replicas, models,
    g_ref, u_ref, d_ref, nv_ref, pg_ref, pu_ref, pd_ref,
    hg_ref, hu_ref, hd_ref, ng_ref, nu_ref, nd_ref, hn_ref, nn_ref,
    pr_g, pr_u, pr_d, r1_g, r1_u, r1_d, r2_g, r2_u, r2_d,
    ow_w, ow_d, hb_g, hb_u, hb_d, nrm_w, nrm_d, zr_w, zr_d, nr, whole,
    ow_sem, pr_send, pr_recv, s1_send, s1_recv, s2_send, s2_recv,
    z_send, z_recv, n_send, n_recv, ag_send, ag_recv, loc_sem, next_sem,
):
    me = lax.axis_index("replica")
    z = lax.axis_index("model")
    k = lax.rem(me, 2)
    x = lax.rem(me // 2, 2)
    y = me // 4
    partner = me + 1 - 2 * k
    xn = me + 2 - 4 * x
    yn = me + 4 - 8 * y
    rate = replicas ** (-0.5)

    slopes = (g_ref, u_ref, d_ref)
    params = (pg_ref, pu_ref, pd_ref)
    halves = (hg_ref, hu_ref, hd_ref)
    nexts = (ng_ref, nu_ref, nd_ref)
    pr, r1, r2 = (pr_g, pr_u, pr_d), (r1_g, r1_u, r1_d), (r2_g, r2_u, r2_d)
    hb = (hb_g, hb_u, hb_d)
    units = 2 * PIECES
    side = pd_ref.shape[1]

    others = [lax.rem(me + d, replicas) for d in range(1, replicas)]
    layers = [lax.rem(z + d, models) for d in range(1, models)]
    barrier = pltpu.get_barrier_semaphore()
    for other in others:
        pl.semaphore_signal(barrier, inc=1, device_id=(other, z), device_id_type=MESH)
    for layer in layers:
        pl.semaphore_signal(barrier, inc=1, device_id=(me, layer), device_id_type=MESH)
    pl.semaphore_wait(barrier, replicas - 1 + models - 1)

    sent = []

    def remote(src, dst, send_sem, recv_sem, to):
        return pltpu.make_async_remote_copy(
            src_ref=src, dst_ref=dst, send_sem=send_sem, recv_sem=recv_sem,
            device_id=to, device_id_type=MESH,
        )

    def start(copy):
        copy.start()
        sent.append(copy)

    def height(m):
        return r2[m].shape[0] // units

    def views(m, u, core):
        rows = pl.ds(u * height(m), height(m))
        if m < 2:
            return [(slopes[m].at[:, :, core, rows, :], None)]
        return [
            (
                slopes[m].at[
                    rows, pl.ds(pl.multiple_of((2 * c + core) * side, side), side)
                ],
                (c // 2, c % 2),
            )
            for c in range(4)
        ]

    def own_copies(m, u):
        ow = ow_w if m < 2 else ow_d
        slot = (m * units + order[u]) % SLOTS
        copies = []
        for n, (src, where) in enumerate(views(m, u, k)):
            dst = ow.at[slot] if where is None else ow.at[slot, where[0], where[1]]
            copies.append(pltpu.make_async_copy(src, dst, ow_sem.at[m, u, n]))
        return copies

    def pair_copies(m, u):
        copies = []
        for n, (src, where) in enumerate(views(m, u, 1 - k)):
            dst = pr[m].at[u] if where is None else pr[m].at[u, where[0], where[1]]
            copies.append(
                remote(src, dst, pr_send.at[m, u, n], pr_recv.at[m, u, n], (partner, z))
            )
        return copies

    sequence = [h * PIECES + j for j in range(PIECES) for h in range(2)]
    order = {u: n for n, u in enumerate(sequence)}
    jobs = [(m, u) for m in range(3) for u in sequence]

    for m, u in jobs[:SLOTS]:
        for copy in own_copies(m, u):
            copy.start()
    for m, u in jobs:
        for copy in pair_copies(m, u):
            start(copy)
    nr[me] = nv_ref[...]
    for n, other in enumerate(others):
        start(remote(nv_ref, nr.at[me], n_send.at[n], n_recv.at[me], (other, z)))

    def first_copy(m, u):
        if u < PIECES:
            src, to = pr[m].at[u, :, 1 - x], xn
        else:
            src, to = pr[m].at[u, 1 - y], yn
        return remote(src, r1[m].at[u], s1_send.at[m, u], s1_recv.at[m, u], (to, z))

    def second_copy(m, u):
        if u < PIECES:
            src, to = r1[m].at[u, 1 - y], yn
        else:
            src, to = r1[m].at[u, 1 - x], xn
        rows = pl.ds(u * height(m), height(m))
        return remote(src, r2[m].at[rows], s2_send.at[m, u], s2_recv.at[m, u], (to, z))

    def stage_1(n):
        m, u = jobs[n]
        ow = ow_w if m < 2 else ow_d
        slot = n % SLOTS
        for copy in own_copies(m, u):
            copy.wait()
        for copy in pair_copies(m, u):
            copy.wait_recv()
        step = tile_rows(r2[m].shape[1])

        @pl.loop(0, height(m) // step)
        def _(i):
            rows = pl.ds(pl.multiple_of(i * step, step), step)
            for a in range(2):
                for b in range(2):
                    pr[m][u, a, b, rows, :] = pr[m][u, a, b, rows, :] + ow[slot, a, b, rows, :]

        start(first_copy(m, u))
        if n + SLOTS < len(jobs):
            for copy in own_copies(*jobs[n + SLOTS]):
                copy.start()

    def stage_2(n):
        m, u = jobs[n]
        first_copy(m, u).wait_recv()
        step = tile_rows(r2[m].shape[1])

        @pl.loop(0, height(m) // step)
        def _(i):
            rows = pl.ds(pl.multiple_of(i * step, step), step)
            for a in range(2):
                kept = pr[m][u, a, x, rows, :] if u < PIECES else pr[m][u, y, a, rows, :]
                r1[m][u, a, rows, :] = r1[m][u, a, rows, :] + kept

        start(second_copy(m, u))

    def lanes(t):
        total = t[:, :128]
        for c in range(1, t.shape[1] // 128):
            total = total + t[:, c * 128 : (c + 1) * 128]
        return total

    def sublanes(t):
        total = t[:8]
        for c in range(1, t.shape[0] // 8):
            total = total + t[c * 8 : (c + 1) * 8]
        return total

    def stage_3(n):
        m, u = jobs[n]
        second_copy(m, u).wait_recv()
        step = tile_rows(r2[m].shape[1])
        kept = y if u < PIECES else x
        if m == 2 and u == sequence[0]:
            nrm_d[...] = jnp.zeros_like(nrm_d)

        @pl.loop(0, height(m) // step)
        def _(i):
            rows = pl.ds(pl.multiple_of(i * step, step), step)
            here = pl.ds(pl.multiple_of(u * height(m) + i * step, step), step)
            mean = (r2[m][here, :] + r1[m][u, kept, rows, :]) * rate
            param = params[m][here, :]
            r2[m][here, :] = mean
            if m < 2:
                nrm_w[m, 0, here, :] = lanes(param * param)
                nrm_w[m, 1, here, :] = lanes(mean * mean)
            else:
                nrm_d[0] = nrm_d[0] + sublanes(param * param)
                nrm_d[1] = nrm_d[1] + sublanes(mean * mean)

    def size_copies(m):
        src = nrm_w.at[m] if m < 2 else nrm_d
        return [
            remote(
                src, zr_w.at[m, n] if m < 2 else zr_d.at[n],
                z_send.at[m, n], z_recv.at[m, n], (me, layer),
            )
            for n, layer in enumerate(layers)
        ]

    def send_sizes(m):
        for copy in size_copies(m):
            start(copy)

    def piece(m, chip, core, h):
        ref = halves[m]
        at = pl.multiple_of((2 * chip + core) * r2[0].shape[0], r2[0].shape[0])
        if m < 2:
            tall = r2[m].shape[0] // 2
            return ref.at[pl.ds(pl.multiple_of(at + h * tall, tall), tall), :]
        tall = r2[m].shape[0] // 2
        at = pl.multiple_of((2 * chip + core) * side, side)
        return ref.at[pl.ds(h * tall, tall), pl.ds(at, side)]

    chip, chip_x, chip_y, chip_d = me // 2, xn // 2, yn // 2, 3 - me // 2

    def gather(m, h, way, src, at, to):
        return remote(src, at, ag_send.at[m, h, way], ag_recv.at[m, h, way], (to, z))

    def await_piece(m, h, way, chip_from, core):
        at = piece(m, chip_from, core, h)
        gather(m, h, way, at, at, partner).wait_recv()
        return at

    local = []

    def update(m):
        for copy in size_copies(m):
            copy.wait_recv()
        step = tile_rows(r2[m].shape[1])
        if m == 2:
            both = nrm_d[...]
            for n in range(models - 1):
                both = both + zr_d[n]
            own = jnp.sum(both[0], axis=0, keepdims=True)
            size = jnp.sum(both[1], axis=0, keepdims=True)
            ratio_d = jnp.sqrt(own) * lax.rsqrt(size + eps)

        step = max(step, 16)

        @pl.loop(0, r2[m].shape[0] // step)
        def _(i):
            rows = pl.ds(pl.multiple_of(i * step, step), step)
            if m < 2:
                own, size = nrm_w[m, 0, rows, :], nrm_w[m, 1, rows, :]
                for n in range(models - 1):
                    own = own + zr_w[m, n, 0, rows, :]
                    size = size + zr_w[m, n, 1, rows, :]
                own = jnp.sum(own, axis=1, keepdims=True)
                size = jnp.sum(size, axis=1, keepdims=True)
                ratio = jnp.sqrt(own) * lax.rsqrt(size + eps)
            else:
                ratio = ratio_d
            new = params[m][rows, :] - learn_rate * (r2[m][rows, :] * ratio)
            r2[m][rows, :] = new
            hb[m][rows, :] = new.astype(bf16)

        copy = pltpu.make_async_copy(r2[m], nexts[m], next_sem.at[m])
        copy.start()
        local.append(copy)
        tall = r2[m].shape[0] // 2
        for h in range(2):
            src = hb[m].at[pl.ds(h * tall, tall)]
            at = piece(m, chip, k, h)
            for way, to in ((1, xn), (2, yn), (0, partner)):
                start(gather(m, h, way, src, at, to))
            copy = pltpu.make_async_copy(src, at, loc_sem.at[m, h])
            copy.start()
            local.append(copy)

    def forward(m):
        at = await_piece(m, 0, 1, chip_x, k)
        start(gather(m, 0, 3, at, at, yn))
        start(gather(m, 0, 4, at, at, partner))
        at = await_piece(m, 1, 2, chip_y, k)
        start(gather(m, 1, 3, at, at, xn))
        start(gather(m, 1, 5, at, at, partner))

    def hand_over(m):
        at = await_piece(m, 1, 1, chip_x, k)
        start(gather(m, 1, 4, at, at, partner))
        at = await_piece(m, 0, 2, chip_y, k)
        start(gather(m, 0, 5, at, at, partner))
        for h in range(2):
            at = await_piece(m, h, 3, chip_d, k)
            start(gather(m, h, 6, at, at, partner))

    steps = len(jobs) // 2
    for t in range(steps + 2):
        for stage, lag in ((stage_1, 0), (stage_2, 1), (stage_3, 2)):
            if 0 <= t - lag < steps:
                for n in (2 * (t - lag), 2 * (t - lag) + 1):
                    stage(n)
        done, rest = divmod(t - 2 + 1, PIECES)
        if t >= 2 and rest == 0 and done >= 1:
            send_sizes(done - 1)
        done, rest = divmod(t - 2, PIECES)
        if t > 2 and rest == 0 and 1 <= done <= 2:
            update(done - 1)
    forward(0)
    update(2)

    for d in range(1, replicas):
        source = lax.rem(me + d, replicas)
        remote(nv_ref, nr.at[source], n_send.at[d - 1], n_recv.at[source], (source, z)).wait_recv()
    tall = hn_ref.shape[0]
    share = nn_ref.shape[0]
    total = nr[0, :tall]
    for n in range(1, replicas):
        total = total + nr[n, :tall]
    for n in range(replicas):
        rows = slice(n * share, (n + 1) * share)
        whole[rows, :] = nr[n, tall : tall + share] - learn_rate * (total[rows] * rate)
    hn_ref[...] = whole[...].astype(bf16)
    nn_ref[...] = whole[pl.ds(me * share, share), :]

    forward(1)
    forward(2)
    for m in range(3):
        hand_over(m)
    for m in range(3):
        for h in range(2):
            await_piece(m, h, 0, chip, 1 - k)
            await_piece(m, h, 4, chip_x, 1 - k)
            await_piece(m, h, 5, chip_y, 1 - k)
            await_piece(m, h, 6, chip_d, 1 - k)
    for copy in local:
        copy.wait()
    for copy in sent:
        copy.wait_send()


def fused(replicas, models):
    def run(
        slope_gate, slope_up, slope_down, slope_norm, param_gate, param_up, param_down, param_norm
    ):
        rows, columns = param_gate.shape
        tall, side = param_down.shape
        units = 2 * PIECES
        tall_n, share = slope_norm.shape[1] // 128, param_norm.shape[0] // 128
        pad = -(tall_n + share) % 8
        vectors = jnp.concatenate(
            [
                slope_norm.reshape(tall_n, 128),
                param_norm.reshape(share, 128),
                jnp.zeros((pad, 128), f32),
            ]
        )
        wide, deep = (rows // units, columns), (tall // units, side)
        V, DMA = pltpu.VMEM, pltpu.SemaphoreType.DMA
        by_chip = (2, replicas // 4, 2, rows, columns)
        shape = jax.ShapeDtypeStruct
        out = pl.pallas_call(
            functools.partial(kernel, replicas, models),
            out_shape=(
                shape((rows * replicas, columns), bf16),
                shape((rows * replicas, columns), bf16),
                shape((tall, side * replicas), bf16),
                shape((rows, columns), f32),
                shape((rows, columns), f32),
                shape((tall, side), f32),
                shape((tall_n, 128), bf16),
                shape((share, 128), f32),
            ),
            in_specs=[pl.BlockSpec(memory_space=pl.ANY)] * 3
            + [pl.BlockSpec(memory_space=pltpu.VMEM)] * 4,
            out_specs=tuple(
                [pl.BlockSpec(memory_space=pl.ANY)] * 6
                + [pl.BlockSpec(memory_space=pltpu.VMEM)] * 2
            ),
            scratch_shapes=[
                V((units, 2, 2) + wide, f32), V((units, 2, 2) + wide, f32), V((units, 2, 2) + deep, f32),
                V((units, 2) + wide, f32), V((units, 2) + wide, f32), V((units, 2) + deep, f32),
                V((rows, columns), f32), V((rows, columns), f32), V((tall, side), f32),
                V((SLOTS, 2, 2) + wide, f32), V((SLOTS, 2, 2) + deep, f32),
                V((rows, columns), bf16), V((rows, columns), bf16), V((tall, side), bf16),
                V((2, 2, rows, 128), f32), V((2, 8, side), f32),
                V((2, models - 1, 2, rows, 128), f32), V((models - 1, 2, 8, side), f32),
                V((replicas,) + vectors.shape, f32), V((tall_n, 128), f32),
                DMA((3, units, 4)), DMA((3, units, 4)), DMA((3, units, 4)),
                DMA((3, units)), DMA((3, units)), DMA((3, units)), DMA((3, units)),
                DMA((3, models - 1)), DMA((3, models - 1)),
                DMA((replicas - 1,)), DMA((replicas,)),
                DMA((3, 2, 7)), DMA((3, 2, 7)), DMA((3, 2)), DMA((3,)),
            ],
            compiler_params=pltpu.CompilerParams(
                collective_id=0, has_side_effects=True, vmem_limit_bytes=67043328
            ),
        )(
            slope_gate.reshape(by_chip), slope_up.reshape(by_chip), slope_down[0],
            vectors, param_gate, param_up, param_down,
        )
        half_gate, half_up, half_down, next_gate, next_up, next_down, half_norm, next_norm = out
        return (
            half_gate, half_up, half_down, half_norm.reshape(-1),
            next_gate, next_up, next_down, next_norm.reshape(-1),
        )

    return run


def plain(
    slope_gate, slope_up, slope_down, slope_norm, param_gate, param_up, param_down, param_norm
):
    rate = lax.axis_size("replica") ** (-0.5)
    halves, nexts = [], []
    for slope, param, dim in (
        (slope_gate, param_gate, 0), (slope_up, param_up, 0), (slope_down, param_down, 1)
    ):
        mean = lax.psum_scatter(slope[0], "replica", scatter_dimension=dim, tiled=True) * rate
        own, size = lax.psum(
            (
                jnp.sum(param * param, axis=1 - dim, keepdims=True),
                jnp.sum(mean * mean, axis=1 - dim, keepdims=True),
            ),
            "model",
        )
        new = param - learn_rate * (mean * (jnp.sqrt(own) * lax.rsqrt(size + eps)))
        nexts.append(new)
        halves.append(lax.all_gather(new.astype(bf16), "replica", axis=dim, tiled=True))
    mean = lax.psum_scatter(slope_norm[0], "replica", scatter_dimension=0, tiled=True) * rate
    new = param_norm - learn_rate * mean
    nexts.append(new)
    halves.append(lax.all_gather(new.astype(bf16), "replica", axis=0, tiled=True))
    return (*halves, *nexts)


def solution(mesh):
    replicas, models = mesh.shape["replica"], mesh.shape["model"]
    body = fused(replicas, models) if replicas == 2 * 2 * 2 else plain
    matrix, turned = P("replica", "model"), P("model", "replica")
    return jax.shard_map(
        body,
        mesh=mesh,
        in_specs=(
            P("replica", None, "model"),
            P("replica", None, "model"),
            P("replica", "model", None),
            P("replica", None),
            matrix, matrix, turned, P("replica"),
        ),
        out_specs=(
            P(None, "model"), P(None, "model"), P("model", None), P(),
            matrix, matrix, turned, P("replica"),
        ),
        check_vma=False,
    )
```

time: 475 us -> 270 us (0.57)
  waiting for transfers between devices: 395 us -> 0 us
  Pallas kernels: 0 us -> 249 us
  blocking collectives: 33.6 us -> 0 us
  other arithmetic: 15.7 us -> 1.38 us
  between operations: 14.2 us -> 0.67 us
    reduce_scatter x3 -> x0, waiting for transfers between devices: 283 us -> none  [the longest x1 94.3 us: body(): lax.psum_scatter(slope_down[0], 'replica', scatter_dimension=1, tiled=True)]
    pallas_call x0 -> x1, Pallas kernels: none -> 249 us  [run(): pl.pallas_call(functools.partial(kernel, replicas, models), out_shape=(sh...]
    all_gather x3 -> x0, waiting for transfers between devices: 110 us -> none  [the longest x1 48.9 us: body(): lax.all_gather(next_down.astype(jnp.bfloat16), 'replica', axis=1, tiled=T...]
    psum x2 -> x0, blocking collectives: 24.6 us -> none  [the longest x1 12.8 us: body(): whole_norm = lax.psum(slope_norm[0], 'replica')]
    convert_element_type x4 -> x0, other arithmetic: 10.1 us -> none  [the longest x1 3.19 us: body(): next_down.astype(jnp.bfloat16)]
    all_gather x1 -> x0, blocking collectives: 8.99 us -> none  [body(): lax.all_gather(next_norm.astype(jnp.bfloat16), 'replica', axis=0, tiled=T...]
    reduce_sum x6 -> x0, other arithmetic: 5.52 us -> none  [the longest x1 1.65 us: body(): jnp.sum(mean_down * mean_down, axis=0, keepdims=True)]
    unnamed x23 -> x22, local copies, waits for them, and re-layouts: 16.3 us -> 18.9 us
  transfers between devices with their start and end apart: 6 -> 0, of which waited for: 6 -> 0; matrix products, arithmetic and copies ran while one was open for 2% -> 0% of each run, Pallas kernels for 0% -> 0%
where the time goes in v1:
time: 270 us
  Pallas kernels  249 us (92%)
  local copies, waits for them, and re-layouts  19 us (7%)
    pallas_call x1, Pallas kernels, run(): pl.pallas_call(functools.partial(kernel, replicas, models), out_shape=(sh...  249 us
    unnamed x22, local copies, waits for them, and re-layouts  18.9 us

profile of v1, /device:TPU:0, one launch (start us, length us, event | category | flops | bytes accessed | tf_op | source)
XLA Modules:
  0.0 269.9 jit_solution(2350671011911266138)
XLA Ops:
  0.6 0.1 pad.2.clone
  0.7 1.4 maximum_maximum_fusion.nv_ref
  2.1 248.8 %shard_map.143 = (bf16[2048,1536]{1,0:T(8,128)(2,1)}, bf16[2048,1536]{1,0:T(8,128)(2,1)}, bf16[1536,2048]{1,0:T(8,128)(2,1)}, f32[256,1536]{1,0:T(8,128)}, f32[2...) custom-call(f32[2,2,2,256,1536]{4,3,2,1,0:T(8,128)} %bitcast.7, ...), custom_call_target="tpu_custom_call" | custom-call | tf_op jit(solution)/shard_map/pallas_call | solution.py:367
  250.9 0.0 copy-start.1
  250.9 6.1 %copy.24 = bf16[2048,1536]{1,0:T(8,128)(2,1)} copy(bf16[2048,1536]{1,0:T(8,128)(2,1)} %get-tuple-element.32) | data formatting | bytes 12582912
  257.0 0.0 copy-done.1
  257.0 0.0 copy-start
  257.0 3.2 %copy.25 = bf16[2048,1536]{1,0:T(8,128)(2,1)} copy(bf16[2048,1536]{1,0:T(8,128)(2,1)S(1)} %copy-done.1) | data formatting | bytes 12582912
  260.2 1.9 copy-done
  262.1 0.0 copy-start.5
  262.1 0.0 copy-start.4
  262.1 0.0 copy-start.3
  262.1 3.2 %copy.26 = bf16[1536,2048]{1,0:T(8,128)(2,1)} copy(bf16[1536,2048]{1,0:T(8,128)(2,1)S(1)} %copy-done) | data formatting | bytes 12582912
  265.3 0.0 copy-done.5
  265.3 0.0 copy-start.2
  265.3 0.0 copy-start.6
  265.3 0.6 copy.27
  265.9 0.0 copy-done.4
  265.9 1.1 copy.28
  267.0 0.0 copy-done.3
  267.0 1.1 copy.29
  268.2 0.0 copy-done.2
  268.2 1.1 copy.30
  269.3 0.0 copy-done.6
  269.3 0.6 copy.31
  (1 shorter events, 0.0 us)
Async XLA Ops:
  250.9 6.1 %copy-start.1 = (bf16[2048,1536]{1,0:T(8,128)(2,1)S(1)}, bf16[2048,1536]{1,0:T(8,128)(2,1)}, u32[]{:S(2)}) copy-start(bf16[2048,1536]{1,0:T(8,128)(2,1)} %get-tuple-element.33) | copy-start | bytes 18874372
  257.0 5.1 %copy-start = (bf16[1536,2048]{1,0:T(8,128)(2,1)S(1)}, bf16[1536,2048]{1,0:T(8,128)(2,1)}, u32[]{:S(2)}) copy-start(bf16[1536,2048]{1,0:T(8,128)(2,1)} %get-tuple-element.34) | copy-start | bytes 18874372
  262.1 3.2 %copy-start.5 = (bf16[16,128]{1,0:T(8,128)(2,1)S(1)}, bf16[16,128]{1,0:T(8,128)(2,1)}, u32[]{:S(2)}) copy-start(bf16[16,128]{1,0:T(8,128)(2,1)} %get-tuple-element.19) | copy-start | bytes 12292
  262.1 3.8 %copy-start.4 = (f32[256,1536]{1,0:T(8,128)S(1)}, f32[256,1536]{1,0:T(8,128)}, u32[]{:S(2)}) copy-start(f32[256,1536]{1,0:T(8,128)} %get-tuple-element.36) | copy-start | bytes 4718596
  262.1 4.9 %copy-start.3 = (f32[256,1536]{1,0:T(8,128)S(1)}, f32[256,1536]{1,0:T(8,128)}, u32[]{:S(2)}) copy-start(f32[256,1536]{1,0:T(8,128)} %get-tuple-element.37) | copy-start | bytes 4718596
  265.3 2.9 %copy-start.2 = (f32[1536,256]{1,0:T(8,128)S(1)}, f32[1536,256]{1,0:T(8,128)}, u32[]{:S(2)}) copy-start(f32[1536,256]{1,0:T(8,128)} %get-tuple-element.38) | copy-start | bytes 4718596
  265.3 4.0 %copy-start.6 = (f32[2,128]{1,0:T(2,128)S(1)}, f32[2,128]{1,0:T(2,128)}, u32[]{:S(2)}) copy-start(f32[2,128]{1,0:T(2,128)} %get-tuple-element.23) | copy-start | bytes 3076

commit v2 on v1

--- a/solution.py
+++ b/solution.py
@@ -11,7 +11,7 @@
 eps = 1e-06
 MESH = pl.DeviceIdType.MESH
 f32, bf16 = jnp.float32, jnp.bfloat16
-PIECES = 2
+PIECES = 4
 SLOTS = 4
 
 
@@ -275,9 +275,12 @@
         tall = r2[m].shape[0] // 2
         for h in range(2):
             src = hb[m].at[pl.ds(h * tall, tall)]
+            start(gather(m, h, 1 + h, src, piece(m, chip, k, h), (xn, yn)[h]))
+        for h in range(2):
+            src = hb[m].at[pl.ds(h * tall, tall)]
             at = piece(m, chip, k, h)
-            for way, to in ((1, xn), (2, yn), (0, partner)):
-                start(gather(m, h, way, src, at, to))
+            start(gather(m, h, 2 - h, src, at, (yn, xn)[h]))
+            start(gather(m, h, 0, src, at, partner))
             copy = pltpu.make_async_copy(src, at, loc_sem.at[m, h])
             copy.start()
             local.append(copy)

time: 270 us -> 272 us (level)
  no operation moved by 1% of the time
where the time goes in v2:
time: 272 us; the launch traced here: 271 us
  Pallas kernels  250 us (92%)
  local copies, waits for them, and re-layouts  19 us (7%)
    pallas_call x1, Pallas kernels, run(): pl.pallas_call(functools.partial(kernel, replicas, models), out_shape=(sh...  250 us
    unnamed x22, local copies, waits for them, and re-layouts  18.9 us

profile of v2, /device:TPU:0, one launch (start us, length us, event | category | flops | bytes accessed | tf_op | source)
XLA Modules:
  0.0 271.4 jit_solution(4051670116201347921)
XLA Ops:
  0.6 0.1 pad.2.clone
  0.7 1.4 maximum_maximum_fusion.nv_ref
  2.1 250.3 %shard_map.143 = (bf16[2048,1536]{1,0:T(8,128)(2,1)}, bf16[2048,1536]{1,0:T(8,128)(2,1)}, bf16[1536,2048]{1,0:T(8,128)(2,1)}, f32[256,1536]{1,0:T(8,128)}, f32[2...) custom-call(f32[2,2,2,256,1536]{4,3,2,1,0:T(8,128)} %bitcast.7, ...), custom_call_target="tpu_custom_call" | custom-call | tf_op jit(solution)/shard_map/pallas_call | solution.py:370
  252.4 0.0 copy-start.1
  252.4 6.1 %copy.24 = bf16[2048,1536]{1,0:T(8,128)(2,1)} copy(bf16[2048,1536]{1,0:T(8,128)(2,1)} %get-tuple-element.32) | data formatting | bytes 12582912
  258.5 0.0 copy-done.1
  258.5 0.0 copy-start
  258.5 3.2 %copy.25 = bf16[2048,1536]{1,0:T(8,128)(2,1)} copy(bf16[2048,1536]{1,0:T(8,128)(2,1)S(1)} %copy-done.1) | data formatting | bytes 12582912
  261.7 1.9 copy-done
  263.6 0.0 copy-start.5
  263.6 0.0 copy-start.4
  263.6 0.0 copy-start.3
  263.6 3.2 %copy.26 = bf16[1536,2048]{1,0:T(8,128)(2,1)} copy(bf16[1536,2048]{1,0:T(8,128)(2,1)S(1)} %copy-done) | data formatting | bytes 12582912
  266.8 0.0 copy-done.5
  266.8 0.0 copy-start.2
  266.8 0.0 copy-start.6
  266.8 0.6 copy.27
  267.4 0.0 copy-done.4
  267.4 1.1 copy.28
  268.5 0.0 copy-done.3
  268.5 1.1 copy.29
  269.7 0.0 copy-done.2
  269.7 1.1 copy.30
  270.8 0.0 copy-done.6
  270.8 0.6 copy.31
  (1 shorter events, 0.0 us)
Async XLA Ops:
  252.4 6.1 %copy-start.1 = (bf16[2048,1536]{1,0:T(8,128)(2,1)S(1)}, bf16[2048,1536]{1,0:T(8,128)(2,1)}, u32[]{:S(2)}) copy-start(bf16[2048,1536]{1,0:T(8,128)(2,1)} %get-tuple-element.33) | copy-start | bytes 18874372
  258.5 5.1 %copy-start = (bf16[1536,2048]{1,0:T(8,128)(2,1)S(1)}, bf16[1536,2048]{1,0:T(8,128)(2,1)}, u32[]{:S(2)}) copy-start(bf16[1536,2048]{1,0:T(8,128)(2,1)} %get-tuple-element.34) | copy-start | bytes 18874372
  263.6 3.2 %copy-start.5 = (bf16[16,128]{1,0:T(8,128)(2,1)S(1)}, bf16[16,128]{1,0:T(8,128)(2,1)}, u32[]{:S(2)}) copy-start(bf16[16,128]{1,0:T(8,128)(2,1)} %get-tuple-element.19) | copy-start | bytes 12292
  263.6 3.8 %copy-start.4 = (f32[256,1536]{1,0:T(8,128)S(1)}, f32[256,1536]{1,0:T(8,128)}, u32[]{:S(2)}) copy-start(f32[256,1536]{1,0:T(8,128)} %get-tuple-element.36) | copy-start | bytes 4718596
  263.6 4.9 %copy-start.3 = (f32[256,1536]{1,0:T(8,128)S(1)}, f32[256,1536]{1,0:T(8,128)}, u32[]{:S(2)}) copy-start(f32[256,1536]{1,0:T(8,128)} %get-tuple-element.37) | copy-start | bytes 4718596
  266.8 2.9 %copy-start.2 = (f32[1536,256]{1,0:T(8,128)S(1)}, f32[1536,256]{1,0:T(8,128)}, u32[]{:S(2)}) copy-start(f32[1536,256]{1,0:T(8,128)} %get-tuple-element.38) | copy-start | bytes 4718596
  266.8 4.0 %copy-start.6 = (f32[2,128]{1,0:T(2,128)S(1)}, f32[2,128]{1,0:T(2,128)}, u32[]{:S(2)}) copy-start(f32[2,128]{1,0:T(2,128)} %get-tuple-element.23) | copy-start | bytes 3076
